TPU v7x, 32 devices: a whole 2x2x4 slice. The times are simulated.
32 devices in a mesh: inst: 4 (over y, core), cells: 8 (over z, x).
Axes of the slice: x: 2, y: 2, z: 4, core: 2. Of those that a mesh axis runs over, the one named last changes fastest.
Arguments:
- flow_state: float32 [8, 5, 64, 32, 128], P('inst', None, 'cells'), may hold values from -6 to 6
- forcing: float32 [8, 5, 64, 32, 128], P('inst', None, 'cells'), may hold values from -6 to 6
- diffusion: float32 [64, 32, 128], P('cells'), may hold values from 0.2 to 0.6
- block_inverse: float32 [5, 5, 64, 32, 128], P(None, None, 'cells', 'inst'), may hold values from -0.03 to 0.15, as said below
Outputs:
- new_state: float32 [8, 5, 64, 32, 128], P('inst', None, 'cells')
Inputs may be any that keep to these rules, and one draw needn't show every extreme that they name: block_inverse[v, v] lies between 0.06 and 0.15; entries off the diagonal lie between -0.03 and 0.03.
All inputs are finite; a program needn't handle non-finite values.
Results may differ from a plain program's by a relative error of at most 0.0001.
Values sent between devices are 32-bit elements; how exact they have to be, the bound alone decides.
A program may use at most 64 MiB of HBM per device.

v0:
```python
import math

import jax
import jax.numpy as jnp
from jax import lax
from jax.sharding import PartitionSpec as P

SWEEPS = 4


frequency = 1.0


def extended(shard, sides, width):
    for axis, dim in sides:
        size, length = (lax.axis_size(axis), shard.shape[dim])
        up = [(i, (i + 1) % size) for i in range(size - 1)]
        down = [(j, i) for i, j in up]
        last = lax.slice_in_dim(shard, length - width, length, axis=dim)
        initial = lax.slice_in_dim(shard, 0, width, axis=dim)
        before = lax.ppermute(last, axis, up)
        after = lax.ppermute(initial, axis, down)
        shard = jnp.concatenate([before, shard, after], axis=dim)
    return shard


def spectral_matrix(count):
    index = jnp.arange(count)
    offset = index[:, None] - index[None, :]
    parity = jnp.where(offset % 2 == 0, 1.0, -1.0)
    angle = math.pi * jnp.where(offset == 0, 1, offset) / count
    entries = 0.5 * parity / jnp.tan(angle)
    return jnp.where(offset == 0, 0.0, entries).astype(jnp.float32)


def interior_sum(padded):
    padded = jnp.pad(padded, ((0, 0), (0, 0), (0, 0), (0, 0), (1, 1)))
    beside = padded[:, :, 2:, 1:-1, 1:-1] + padded[:, :, :-2, 1:-1, 1:-1]
    beside = beside + padded[:, :, 1:-1, 2:, 1:-1] + padded[:, :, 1:-1, :-2, 1:-1]
    beside = beside + padded[:, :, 1:-1, 1:-1, 2:] + padded[:, :, 1:-1, 1:-1, :-2]
    return beside


def block_neighbours(grid_field):
    padded = extended(grid_field, (("inst", 3), ("cells", 2)), 1)
    return interior_sum(padded)


def spectral_term(matrix, grid_field):
    flat = grid_field.reshape(grid_field.shape[0], -1)
    product = jnp.dot(matrix, flat, precision=lax.Precision.HIGHEST)
    return (frequency * product).reshape(grid_field.shape)


def apply_blocks(block_inverse, source):
    outputs = []
    for row_index in range(block_inverse.shape[0]):
        total = block_inverse[row_index, 0][None] * source[:, 0]
        for col_index in range(1, block_inverse.shape[1]):
            total = total + block_inverse[row_index, col_index][None] * source[:, col_index]
        outputs.append(total)
    return jnp.stack(outputs, axis=1)


def on_device(flow_state, forcing, diffusion, block_inverse):
    block_rows = block_inverse.shape[3]
    first_row = lax.axis_index("inst") * block_rows
    weight_block = lax.dynamic_slice_in_dim(diffusion, first_row, block_rows, 1)[None, None]
    matrix = spectral_matrix(lax.axis_size("inst") * flow_state.shape[0])
    padded = extended(flow_state, (("cells", 2),), 1)
    padded = jnp.pad(padded, ((0, 0), (0, 0), (0, 0), (1, 1), (0, 0)))
    local_part = diffusion[None, None] * (6.0 * flow_state - interior_sum(padded)) - forcing
    moved_state, moved_part = (
        lax.all_to_all(flow_state, "inst", split_axis=3, concat_axis=0, tiled=True),
        lax.all_to_all(local_part, "inst", split_axis=3, concat_axis=0, tiled=True),
    )
    residual = moved_part + spectral_term(matrix, moved_state)
    update = apply_blocks(block_inverse, -residual)
    for sweep_index in range(SWEEPS):
        source = -residual - spectral_term(matrix, update) + weight_block * block_neighbours(update)
        update = apply_blocks(block_inverse, source)
    return lax.all_to_all(moved_state + update, "inst", split_axis=0, concat_axis=3, tiled=True)


def solution(mesh):
    in_specs = (
        P("inst", None, "cells", None, None),
        P("inst", None, "cells", None, None),
        P("cells", None, None),
        P(None, None, "cells", "inst", None),
    )
    out_specs = P("inst", None, "cells", None, None)
    return jax.shard_map(
        on_device, mesh=mesh, in_specs=in_specs, out_specs=out_specs, check_vma=False
    )
```

profile of v0, /device:TPU:19, one launch (start us, length us, event | category | flops | bytes accessed | tf_op | source)
XLA Modules:
  0.0 181.7 jit_solution(11460393228800454385)
XLA Ops:
  0.0 3.1 %copy.21 = f32[2,5,8,32,128]{4,2,1,0,3:T(8,128)} copy(f32[2,5,8,32,128]{4,3,2,1,0:T(8,128)} %param.4) | data formatting | bytes 2621440 | tf_op args[0]
  3.1 4.3 %all-to-all-start = ((f32[2,5,8,32,128]{4,2,1,0,3:T(8,128)}), f32[2,5,8,32,128]{4,2,1,0,3:T(8,128)S(1)}, u32[]{:S(2)}, u32[]{:S(2)}) async-start(f32[2,5,8,32,128]{4,2,1,0,3:T(8,128)} %copy.21), calls=%async_computation | async-start | bytes 2621440 | tf_op jit(solution)/shard_map/all_to_all | solution.py:74
  8.5 3.2 %collective-permute-start.1 = (f32[2,5,1,32,128]{4,3,2,1,0:T(8,128)S(1)}, f32[2,5,1,32,128]{4,3,2,1,0:T(8,128)S(1)}, u32[]{:S(2)}, u32[]{:S(2)}) collective-permute-start(f32[2,5,1,32,128]{4,3,2,1,0:T(8,128)S(1)} %get-tuple-element.21), channel_id=1, source_target_pairs={{0,1},{1,2},{2,3},{3,4},{4,5},{5,6},{6,7},{8,9},{9,10},{10,11},{11... | collective-permute-start | bytes 491528 | tf_op jit(solution)/shard_map/ppermute | solution.py:21
  16.2 3.6 %collective-permute-done = f32[2,5,1,32,128]{4,3,2,1,0:T(8,128)S(1)} collective-permute-done((f32[2,5,1,32,128]{4,3,2,1,0:T(8,128)S(1)}, f32[2,5,1,32,128]{4,3,2,1,0:T(8,128)S(1)}, u32[]{:S(2)}, u32[]{:S(2)}) %collective-permute-start) | collective-permute-done | bytes 163872 | tf_op jit(solution)/shard_map/ppermute | solution.py:22
  22.0 5.4 %fusion.7 = f32[2,5,8,32,128]{4,2,1,0,3:T(8,128)} fusion(f32[2,5,10,34,128]{4,2,1,0,3:T(8,128)S(1)} %select_maximum_fusion.16, f32[2,5,8,32,128]{4,2,1,0,3:T(8,128)} %copy.21, f32[2,5,1,32,128]{4,2,1,0,3:T(1,128)S(1)} %copy.27, f32[2,5,1,32,128]{4,2,1,0,3:T(1,128)S(1)} %copy.26, f32[2,5,8,32,128]{4,3,2,1,0:T(8,128)S(1)} %copy-done.2, f32[8,32,128]{2,0,1:T(8,128)S(1)} %copy.23), kind=kLoop, calls=%fused_computation.36 | loop fusion | flops 3604480 | bytes 9797632 | tf_op jit(solution)/shard_map/sub | solution.py:72
  27.4 5.6 %all-to-all-start.1 = ((f32[2,5,8,32,128]{4,2,1,0,3:T(8,128)}), f32[2,5,8,32,128]{4,2,1,0,3:T(8,128)}, u32[]{:S(2)}, u32[]{:S(2)}) async-start(f32[2,5,8,32,128]{4,2,1,0,3:T(8,128)} %fusion.7), calls=%async_computation.1 | async-start | bytes 2621440 | tf_op jit(solution)/shard_map/all_to_all | solution.py:75
  33.7 15.6 %all-to-all-done.1 = f32[2,5,8,32,128]{4,2,1,0,3:T(8,128)} async-done(((f32[2,5,8,32,128]{4,2,1,0,3:T(8,128)}), f32[2,5,8,32,128]{4,2,1,0,3:T(8,128)}, u32[]{:S(2)}, u32[]{:S(2)}) %all-to-all-start.1) | async-done | bytes 1310752 | tf_op jit(solution)/shard_map/all_to_all | solution.py:75
  53.5 2.9 %collective-permute-start.2 = (f32[8,5,8,1,128]{4,0,3,2,1:T(8,128)S(1)}, f32[8,5,8,1,128]{4,0,3,2,1:T(8,128)S(1)}, u32[]{:S(2)}, u32[]{:S(2)}) collective-permute-start(f32[8,5,8,1,128]{4,0,3,2,1:T(8,128)S(1)} %get-tuple-element.19), channel_id=1, source_target_pairs={{0,8},{8,16},{16,24},{1,9},{9,17},{17,25},{2,10},{10,18},{18,26},{... | collective-permute-start | bytes 491528 | tf_op jit(solution)/shard_map/ppermute | solution.py:21
  58.6 4.4 %collective-permute-done.3 = f32[8,5,8,1,128]{4,0,3,2,1:T(8,128)S(1)} collective-permute-done((f32[8,5,8,1,128]{4,0,3,2,1:T(8,128)S(1)}, f32[8,5,8,1,128]{4,0,3,2,1:T(8,128)S(1)}, u32[]{:S(2)}, u32[]{:S(2)}) %collective-permute-start.3) | collective-permute-done | bytes 163872 | tf_op jit(solution)/shard_map/ppermute | solution.py:22
  63.8 3.5 %collective-permute-start.5 = (f32[8,5,1,10,128]{4,0,3,2,1:T(8,128)}, f32[8,5,1,10,128]{4,0,3,2,1:T(8,128)}, u32[]{:S(2)}, u32[]{:S(2)}) collective-permute-start(f32[8,5,1,10,128]{4,0,3,2,1:T(8,128)} %get-tuple-element.11), channel_id=1, source_target_pairs={{0,1},{1,2},{2,3},{3,4},{4,5},{5,6},{6,7},{8,9},{9,10},{10,11},{11... | collective-permute-start | bytes 614408 | tf_op jit(solution)/shard_map/ppermute | solution.py:21
  75.1 4.1 %select_maximum_fusion.12 = f32[8,5,10,10,130]{4,0,3,2,1:T(8,128)S(1)} fusion(f32[8,5,1,10,128]{4,0,3,2,1:T(8,128)} %collective-permute-done.4, f32[8,5,1,10,128]{4,0,3,2,1:T(8,128)} %collective-permute-done.5, f32[8,5,8,1,128]{4,0,3,2,1:T(8,128)} %copy-done.6, f32[8,5,8,8,128]{4,0,3,2,1:T(8,128)} %copy-done, f32[8,5,8,1,128]{4,0,3,2,1:T(8,128)} %copy-done.4), kind=kLoop, calls=%fused_computation.18 | loop fusion | flops 6240000 | bytes 4128000 | tf_op jit(solution)/shard_map/concatenate | solution.py:23
  79.2 3.0 %fusion.24 = f32[8,5,8,8,128]{4,0,3,2,1:T(8,128)S(1)} fusion(f32[8,5,10,10,130]{4,0,3,2,1:T(8,128)S(1)} %select_maximum_fusion.12, f32[8,5,8,8,128]{4,0,3,2,1:T(8,128)S(1)} %copy-done.1, f32[8,5,8,1,128]{4,0,3,2,1:T(8,128)S(1)} %copy-done.5, f32[8,5,8,1,128]{4,0,3,2,1:T(8,128)S(1)} %copy-done.7, f32[8,5,1,10,128]{4,0,3,2,1:T(8,128)} %collective-permute-done.5, ...), kind=kOutput, calls=%fused_computation.84 | convolution fusion | flops 36701504 | bytes 8634368 | tf_op jit(solution)/shard_map/dot_general | solution.py:51
  83.2 3.2 %collective-permute-start.6 = (f32[8,5,8,1,128]{4,0,3,2,1:T(8,128)S(1)}, f32[8,5,8,1,128]{4,0,3,2,1:T(8,128)S(1)}, u32[]{:S(2)}, u32[]{:S(2)}) collective-permute-start(f32[8,5,8,1,128]{4,0,3,2,1:T(8,128)S(1)} %get-tuple-element.17), channel_id=1, source_target_pairs={{0,8},{8,16},{16,24},{1,9},{9,17},{17,25},{2,10},{10,18},{18,26},{... | collective-permute-start | bytes 491528 | tf_op jit(solution)/shard_map/ppermute | solution.py:21
  88.6 4.4 %collective-permute-done.7 = f32[8,5,8,1,128]{4,0,3,2,1:T(8,128)S(1)} collective-permute-done((f32[8,5,8,1,128]{4,0,3,2,1:T(8,128)S(1)}, f32[8,5,8,1,128]{4,0,3,2,1:T(8,128)S(1)}, u32[]{:S(2)}, u32[]{:S(2)}) %collective-permute-start.7) | collective-permute-done | bytes 163872 | tf_op jit(solution)/shard_map/ppermute | solution.py:22
  95.5 2.9 %collective-permute-start.8 = (f32[8,5,1,10,128]{4,0,3,2,1:T(8,128)S(1)}, f32[8,5,1,10,128]{4,0,3,2,1:T(8,128)S(1)}, u32[]{:S(2)}, u32[]{:S(2)}) collective-permute-start(f32[8,5,1,10,128]{4,0,3,2,1:T(8,128)S(1)} %get-tuple-element.10), channel_id=1, source_target_pairs={{1,0},{2,1},{3,2},{4,3},{5,4},{6,5},{7,6},{9,8},{10,9},{11,10},{12... | collective-permute-start | bytes 614408 | tf_op jit(solution)/shard_map/ppermute | solution.py:22
  98.4 5.6 %collective-permute-done.9 = f32[8,5,1,10,128]{4,0,3,2,1:T(8,128)S(1)} collective-permute-done((f32[8,5,1,10,128]{4,0,3,2,1:T(8,128)S(1)}, f32[8,5,1,10,128]{4,0,3,2,1:T(8,128)S(1)}, u32[]{:S(2)}, u32[]{:S(2)}) %collective-permute-start.9) | collective-permute-done | bytes 204832 | tf_op jit(solution)/shard_map/ppermute | solution.py:21
  114.2 4.4 %collective-permute-done.11 = f32[8,5,8,1,128]{4,0,3,2,1:T(8,128)S(1)} collective-permute-done((f32[8,5,8,1,128]{4,0,3,2,1:T(8,128)S(1)}, f32[8,5,8,1,128]{4,0,3,2,1:T(8,128)S(1)}, u32[]{:S(2)}, u32[]{:S(2)}) %collective-permute-start.11) | collective-permute-done | bytes 163872 | tf_op jit(solution)/shard_map/ppermute | solution.py:22
  118.6 3.0 %collective-permute-start.13 = (f32[8,5,1,10,128]{4,0,3,2,1:T(8,128)S(1)}, f32[8,5,1,10,128]{4,0,3,2,1:T(8,128)S(1)}, u32[]{:S(2)}, u32[]{:S(2)}) collective-permute-start(f32[8,5,1,10,128]{4,0,3,2,1:T(8,128)S(1)} %get-tuple-element.7), channel_id=1, source_target_pairs={{0,1},{1,2},{2,3},{3,4},{4,5},{5,6},{6,7},{8,9},{9,10},{10,11},{11... | collective-permute-start | bytes 614408 | tf_op jit(solution)/shard_map/ppermute | solution.py:21
  124.1 5.4 %collective-permute-done.13 = f32[8,5,1,10,128]{4,0,3,2,1:T(8,128)S(1)} collective-permute-done((f32[8,5,1,10,128]{4,0,3,2,1:T(8,128)S(1)}, f32[8,5,1,10,128]{4,0,3,2,1:T(8,128)S(1)}, u32[]{:S(2)}, u32[]{:S(2)}) %collective-permute-start.13) | collective-permute-done | bytes 204832 | tf_op jit(solution)/shard_map/ppermute | solution.py:21
  140.3 4.4 %collective-permute-done.15 = f32[8,5,8,1,128]{4,0,3,2,1:T(8,128)S(1)} collective-permute-done((f32[8,5,8,1,128]{4,0,3,2,1:T(8,128)S(1)}, f32[8,5,8,1,128]{4,0,3,2,1:T(8,128)S(1)}, u32[]{:S(2)}, u32[]{:S(2)}) %collective-permute-start.15) | collective-permute-done | bytes 163872 | tf_op jit(solution)/shard_map/ppermute | solution.py:22
  144.8 3.0 %collective-permute-start.17 = (f32[8,5,1,10,128]{4,0,3,2,1:T(8,128)S(1)}, f32[8,5,1,10,128]{4,0,3,2,1:T(8,128)S(1)}, u32[]{:S(2)}, u32[]{:S(2)}) collective-permute-start(f32[8,5,1,10,128]{4,0,3,2,1:T(8,128)S(1)} %get-tuple-element.5), channel_id=1, source_target_pairs={{0,1},{1,2},{2,3},{3,4},{4,5},{5,6},{6,7},{8,9},{9,10},{10,11},{11... | collective-permute-start | bytes 614408 | tf_op jit(solution)/shard_map/ppermute | solution.py:21
  150.1 5.6 %collective-permute-done.17 = f32[8,5,1,10,128]{4,0,3,2,1:T(8,128)S(1)} collective-permute-done((f32[8,5,1,10,128]{4,0,3,2,1:T(8,128)S(1)}, f32[8,5,1,10,128]{4,0,3,2,1:T(8,128)S(1)}, u32[]{:S(2)}, u32[]{:S(2)}) %collective-permute-start.17) | collective-permute-done | bytes 204832 | tf_op jit(solution)/shard_map/ppermute | solution.py:21
  155.7 2.8 %select_maximum_fusion = f32[8,5,10,10,130]{4,0,3,2,1:T(8,128)S(1)} fusion(f32[8,5,1,10,128]{4,0,3,2,1:T(8,128)S(1)} %collective-permute-done.16, f32[8,5,1,10,128]{4,0,3,2,1:T(8,128)S(1)} %collective-permute-done.17, f32[8,5,8,1,128]{4,0,3,2,1:T(8,128)S(1)} %collective-permute-done.15, f32[8,5,8,8,128]{4,0,3,2,1:T(8,128)S(1)} %add_dynamic-update-slice_fusion.5, ...), kind=kLoop, calls=%fused_computation.6 | loop fusion | flops 6240000 | bytes 4128000 | tf_op jit(solution)/shard_map/concatenate | solution.py:23
  162.0 18.5 %all_to_all.54 = f32[8,5,8,8,128]{4,3,2,1,0:T(8,128)S(1)} all-to-all(f32[8,5,8,8,128]{4,3,2,1,0:T(8,128)S(1)} %copy.34), channel_id=1, replica_groups=mesh['inst'=4,'cells'=8] {'inst'}, dimensions={0} | all-to-all | bytes 2621440 | tf_op jit(solution)/shard_map/all_to_all | solution.py:82
  (92 shorter events, 59.3 us)
Async XLA Ops:
  3.1 10.6 %copy-start.8 = (f32[8,32,128]{2,1,0:T(8,128)S(1)}, f32[8,32,128]{2,1,0:T(8,128)}, u32[]{:S(2)}) copy-start(f32[8,32,128]{2,1,0:T(8,128)} %param.6) | copy-start | bytes 393220
  3.1 24.3 %all-to-all-start = ((f32[2,5,8,32,128]{4,2,1,0,3:T(8,128)}), f32[2,5,8,32,128]{4,2,1,0,3:T(8,128)S(1)}, u32[]{:S(2)}, u32[]{:S(2)}) async-start(f32[2,5,8,32,128]{4,2,1,0,3:T(8,128)} %copy.21), calls=%async_computation | async-start | bytes 2621440 | tf_op jit(solution)/shard_map/all_to_all | solution.py:74
  8.5 7.6 %collective-permute-start.1 = (f32[2,5,1,32,128]{4,3,2,1,0:T(8,128)S(1)}, f32[2,5,1,32,128]{4,3,2,1,0:T(8,128)S(1)}, u32[]{:S(2)}, u32[]{:S(2)}) collective-permute-start(f32[2,5,1,32,128]{4,3,2,1,0:T(8,128)S(1)} %get-tuple-element.21), channel_id=1, source_target_pairs={{0,1},{1,2},{2,3},{3,4},{4,5},{5,6},{6,7},{8,9},{9,10},{10,11},{11... | collective-permute-start | bytes 491528 | tf_op jit(solution)/shard_map/ppermute | solution.py:21
  11.7 8.2 %collective-permute-start = (f32[2,5,1,32,128]{4,3,2,1,0:T(8,128)S(1)}, f32[2,5,1,32,128]{4,3,2,1,0:T(8,128)S(1)}, u32[]{:S(2)}, u32[]{:S(2)}) collective-permute-start(f32[2,5,1,32,128]{4,3,2,1,0:T(8,128)S(1)} %get-tuple-element.22), channel_id=1, source_target_pairs={{1,0},{2,1},{3,2},{4,3},{5,4},{6,5},{7,6},{9,8},{10,9},{11,10},{12... | collective-permute-start | bytes 491528 | tf_op jit(solution)/shard_map/ppermute | solution.py:22
  27.4 22.0 %all-to-all-start.1 = ((f32[2,5,8,32,128]{4,2,1,0,3:T(8,128)}), f32[2,5,8,32,128]{4,2,1,0,3:T(8,128)}, u32[]{:S(2)}, u32[]{:S(2)}) async-start(f32[2,5,8,32,128]{4,2,1,0,3:T(8,128)} %fusion.7), calls=%async_computation.1 | async-start | bytes 2621440 | tf_op jit(solution)/shard_map/all_to_all | solution.py:75
  53.4 10.4 %copy-start = (f32[8,5,8,8,128]{4,0,3,2,1:T(8,128)}, f32[8,5,8,8,128]{4,0,3,2,1:T(8,128)S(1)}, u32[]{:S(2)}) copy-start(f32[8,5,8,8,128]{4,0,3,2,1:T(8,128)S(1)} %add_dynamic-update-slice_fusion.20) | copy-start | bytes 3932164
  53.5 5.1 %collective-permute-start.2 = (f32[8,5,8,1,128]{4,0,3,2,1:T(8,128)S(1)}, f32[8,5,8,1,128]{4,0,3,2,1:T(8,128)S(1)}, u32[]{:S(2)}, u32[]{:S(2)}) collective-permute-start(f32[8,5,8,1,128]{4,0,3,2,1:T(8,128)S(1)} %get-tuple-element.19), channel_id=1, source_target_pairs={{0,8},{8,16},{16,24},{1,9},{9,17},{17,25},{2,10},{10,18},{18,26},{... | collective-permute-start | bytes 491528 | tf_op jit(solution)/shard_map/ppermute | solution.py:21
  56.4 6.6 %collective-permute-start.3 = (f32[8,5,8,1,128]{4,0,3,2,1:T(8,128)S(1)}, f32[8,5,8,1,128]{4,0,3,2,1:T(8,128)S(1)}, u32[]{:S(2)}, u32[]{:S(2)}) collective-permute-start(f32[8,5,8,1,128]{4,0,3,2,1:T(8,128)S(1)} %get-tuple-element.20), channel_id=1, source_target_pairs={{8,0},{16,8},{24,16},{9,1},{17,9},{25,17},{10,2},{18,10},{26,18},{... | collective-permute-start | bytes 491528 | tf_op jit(solution)/shard_map/ppermute | solution.py:22
  63.8 9.0 %collective-permute-start.5 = (f32[8,5,1,10,128]{4,0,3,2,1:T(8,128)}, f32[8,5,1,10,128]{4,0,3,2,1:T(8,128)}, u32[]{:S(2)}, u32[]{:S(2)}) collective-permute-start(f32[8,5,1,10,128]{4,0,3,2,1:T(8,128)} %get-tuple-element.11), channel_id=1, source_target_pairs={{0,1},{1,2},{2,3},{3,4},{4,5},{5,6},{6,7},{8,9},{9,10},{10,11},{11... | collective-permute-start | bytes 614408 | tf_op jit(solution)/shard_map/ppermute | solution.py:21
  67.4 7.7 %collective-permute-start.4 = (f32[8,5,1,10,128]{4,0,3,2,1:T(8,128)}, f32[8,5,1,10,128]{4,0,3,2,1:T(8,128)}, u32[]{:S(2)}, u32[]{:S(2)}) collective-permute-start(f32[8,5,1,10,128]{4,0,3,2,1:T(8,128)} %get-tuple-element.12), channel_id=1, source_target_pairs={{1,0},{2,1},{3,2},{4,3},{5,4},{6,5},{7,6},{9,8},{10,9},{11,10},{12... | collective-permute-start | bytes 614408 | tf_op jit(solution)/shard_map/ppermute | solution.py:22
  70.2 9.0 %copy-start.5 = (f32[8,5,8,1,128]{4,0,3,2,1:T(8,128)S(1)}, f32[8,5,8,1,128]{4,0,3,2,1:T(8,128)}, u32[]{:S(2)}) copy-start(f32[8,5,8,1,128]{4,0,3,2,1:T(8,128)} %copy-done.4) | copy-start | bytes 491524
  70.2 9.0 %copy-start.7 = (f32[8,5,8,1,128]{4,0,3,2,1:T(8,128)S(1)}, f32[8,5,8,1,128]{4,0,3,2,1:T(8,128)}, u32[]{:S(2)}) copy-start(f32[8,5,8,1,128]{4,0,3,2,1:T(8,128)} %copy-done.6) | copy-start | bytes 491524
  83.2 5.4 %collective-permute-start.6 = (f32[8,5,8,1,128]{4,0,3,2,1:T(8,128)S(1)}, f32[8,5,8,1,128]{4,0,3,2,1:T(8,128)S(1)}, u32[]{:S(2)}, u32[]{:S(2)}) collective-permute-start(f32[8,5,8,1,128]{4,0,3,2,1:T(8,128)S(1)} %get-tuple-element.17), channel_id=1, source_target_pairs={{0,8},{8,16},{16,24},{1,9},{9,17},{17,25},{2,10},{10,18},{18,26},{... | collective-permute-start | bytes 491528 | tf_op jit(solution)/shard_map/ppermute | solution.py:21
  86.4 6.6 %collective-permute-start.7 = (f32[8,5,8,1,128]{4,0,3,2,1:T(8,128)S(1)}, f32[8,5,8,1,128]{4,0,3,2,1:T(8,128)S(1)}, u32[]{:S(2)}, u32[]{:S(2)}) collective-permute-start(f32[8,5,8,1,128]{4,0,3,2,1:T(8,128)S(1)} %get-tuple-element.18), channel_id=1, source_target_pairs={{8,0},{16,8},{24,16},{9,1},{17,9},{25,17},{10,2},{18,10},{26,18},{... | collective-permute-start | bytes 491528 | tf_op jit(solution)/shard_map/ppermute | solution.py:22
  93.1 10.9 %collective-permute-start.9 = (f32[8,5,1,10,128]{4,0,3,2,1:T(8,128)S(1)}, f32[8,5,1,10,128]{4,0,3,2,1:T(8,128)S(1)}, u32[]{:S(2)}, u32[]{:S(2)}) collective-permute-start(f32[8,5,1,10,128]{4,0,3,2,1:T(8,128)S(1)} %get-tuple-element.9), channel_id=1, source_target_pairs={{0,1},{1,2},{2,3},{3,4},{4,5},{5,6},{6,7},{8,9},{9,10},{10,11},{11... | collective-permute-start | bytes 614408 | tf_op jit(solution)/shard_map/ppermute | solution.py:21
  95.5 8.5 %collective-permute-start.8 = (f32[8,5,1,10,128]{4,0,3,2,1:T(8,128)S(1)}, f32[8,5,1,10,128]{4,0,3,2,1:T(8,128)S(1)}, u32[]{:S(2)}, u32[]{:S(2)}) collective-permute-start(f32[8,5,1,10,128]{4,0,3,2,1:T(8,128)S(1)} %get-tuple-element.10), channel_id=1, source_target_pairs={{1,0},{2,1},{3,2},{4,3},{5,4},{6,5},{7,6},{9,8},{10,9},{11,10},{12... | collective-permute-start | bytes 614408 | tf_op jit(solution)/shard_map/ppermute | solution.py:22
  109.8 4.4 %collective-permute-start.10 = (f32[8,5,8,1,128]{4,0,3,2,1:T(8,128)S(1)}, f32[8,5,8,1,128]{4,0,3,2,1:T(8,128)S(1)}, u32[]{:S(2)}, u32[]{:S(2)}) collective-permute-start(f32[8,5,8,1,128]{4,0,3,2,1:T(8,128)S(1)} %get-tuple-element.15), channel_id=1, source_target_pairs={{0,8},{8,16},{16,24},{1,9},{9,17},{17,25},{2,10},{10,18},{18,26},{... | collective-permute-start | bytes 491528 | tf_op jit(solution)/shard_map/ppermute | solution.py:21
  111.9 6.6 %collective-permute-start.11 = (f32[8,5,8,1,128]{4,0,3,2,1:T(8,128)S(1)}, f32[8,5,8,1,128]{4,0,3,2,1:T(8,128)S(1)}, u32[]{:S(2)}, u32[]{:S(2)}) collective-permute-start(f32[8,5,8,1,128]{4,0,3,2,1:T(8,128)S(1)} %get-tuple-element.16), channel_id=1, source_target_pairs={{8,0},{16,8},{24,16},{9,1},{17,9},{25,17},{10,2},{18,10},{26,18},{... | collective-permute-start | bytes 491528 | tf_op jit(solution)/shard_map/ppermute | solution.py:22
  118.6 10.9 %collective-permute-start.13 = (f32[8,5,1,10,128]{4,0,3,2,1:T(8,128)S(1)}, f32[8,5,1,10,128]{4,0,3,2,1:T(8,128)S(1)}, u32[]{:S(2)}, u32[]{:S(2)}) collective-permute-start(f32[8,5,1,10,128]{4,0,3,2,1:T(8,128)S(1)} %get-tuple-element.7), channel_id=1, source_target_pairs={{0,1},{1,2},{2,3},{3,4},{4,5},{5,6},{6,7},{8,9},{9,10},{10,11},{11... | collective-permute-start | bytes 614408 | tf_op jit(solution)/shard_map/ppermute | solution.py:21
  121.7 7.8 %collective-permute-start.12 = (f32[8,5,1,10,128]{4,0,3,2,1:T(8,128)S(1)}, f32[8,5,1,10,128]{4,0,3,2,1:T(8,128)S(1)}, u32[]{:S(2)}, u32[]{:S(2)}) collective-permute-start(f32[8,5,1,10,128]{4,0,3,2,1:T(8,128)S(1)} %get-tuple-element.8), channel_id=1, source_target_pairs={{1,0},{2,1},{3,2},{4,3},{5,4},{6,5},{7,6},{9,8},{10,9},{11,10},{12... | collective-permute-start | bytes 614408 | tf_op jit(solution)/shard_map/ppermute | solution.py:22
  135.4 5.0 %collective-permute-start.14 = (f32[8,5,8,1,128]{4,0,3,2,1:T(8,128)S(1)}, f32[8,5,8,1,128]{4,0,3,2,1:T(8,128)S(1)}, u32[]{:S(2)}, u32[]{:S(2)}) collective-permute-start(f32[8,5,8,1,128]{4,0,3,2,1:T(8,128)S(1)} %get-tuple-element.13), channel_id=1, source_target_pairs={{0,8},{8,16},{16,24},{1,9},{9,17},{17,25},{2,10},{10,18},{18,26},{... | collective-permute-start | bytes 491528 | tf_op jit(solution)/shard_map/ppermute | solution.py:21
  138.1 6.6 %collective-permute-start.15 = (f32[8,5,8,1,128]{4,0,3,2,1:T(8,128)S(1)}, f32[8,5,8,1,128]{4,0,3,2,1:T(8,128)S(1)}, u32[]{:S(2)}, u32[]{:S(2)}) collective-permute-start(f32[8,5,8,1,128]{4,0,3,2,1:T(8,128)S(1)} %get-tuple-element.14), channel_id=1, source_target_pairs={{8,0},{16,8},{24,16},{9,1},{17,9},{25,17},{10,2},{18,10},{26,18},{... | collective-permute-start | bytes 491528 | tf_op jit(solution)/shard_map/ppermute | solution.py:22
  144.8 10.9 %collective-permute-start.17 = (f32[8,5,1,10,128]{4,0,3,2,1:T(8,128)S(1)}, f32[8,5,1,10,128]{4,0,3,2,1:T(8,128)S(1)}, u32[]{:S(2)}, u32[]{:S(2)}) collective-permute-start(f32[8,5,1,10,128]{4,0,3,2,1:T(8,128)S(1)} %get-tuple-element.5), channel_id=1, source_target_pairs={{0,1},{1,2},{2,3},{3,4},{4,5},{5,6},{6,7},{8,9},{9,10},{10,11},{11... | collective-permute-start | bytes 614408 | tf_op jit(solution)/shard_map/ppermute | solution.py:21
  147.8 7.8 %collective-permute-start.16 = (f32[8,5,1,10,128]{4,0,3,2,1:T(8,128)S(1)}, f32[8,5,1,10,128]{4,0,3,2,1:T(8,128)S(1)}, u32[]{:S(2)}, u32[]{:S(2)}) collective-permute-start(f32[8,5,1,10,128]{4,0,3,2,1:T(8,128)S(1)} %get-tuple-element.6), channel_id=1, source_target_pairs={{1,0},{2,1},{3,2},{4,3},{5,4},{6,5},{7,6},{9,8},{10,9},{11,10},{12... | collective-permute-start | bytes 614408 | tf_op jit(solution)/shard_map/ppermute | solution.py:22
  (5 other events, 26.0 us)
where the time goes:
time: 185 us; the launch traced here: 182 us
  waiting for transfers between devices  61.4 us (33%)
  starting transfers between devices  55.7 us (30%)
  other arithmetic  25.7 us (14%)
  blocking collectives  18.5 us (10%)
  matrix products  10.2 us (6%)
  local copies, waits for them, and re-layouts  9.69 us (5%)
    ppermute x9, starting transfers between devices, extended(): before = lax.ppermute(last, axis, up)  26.1 us
    ppermute x9, waiting for transfers between devices, extended(): after = lax.ppermute(initial, axis, down)  23.4 us
    ppermute x9, waiting for transfers between devices, extended(): before = lax.ppermute(last, axis, up)  22.3 us
    ppermute x9, starting transfers between devices, extended(): after = lax.ppermute(initial, axis, down)  19.7 us
    all_to_all x1, blocking collectives, on_device(): lax.all_to_all(moved_state + update, 'inst', split_axis=0, concat_axis=3,...  18.5 us
    all_to_all x1, waiting for transfers between devices, on_device(): lax.all_to_all(local_part, 'inst', split_axis=3, concat_axis=0, tiled=True)  15.6 us
    concatenate x9, other arithmetic, extended(): shard = jnp.concatenate([before, shard, after], axis=dim)  15.4 us
    dot_general x5, matrix products, spectral_term(): product = jnp.dot(matrix, flat, precision=lax.Precision.HIGHEST)  10.2 us
  transfers between devices with their start and end apart: 20, of which 15 were waited for; matrix products, arithmetic and copies ran while one was open for 6% of the time, Pallas kernels for 0%

commit v1 on v0

v1 whole, which is shorter than its diff:
```python
import functools
import math

import jax
import jax.numpy as jnp
from jax import lax
from jax.experimental import pallas as pl
from jax.experimental.pallas import tpu as pltpu
from jax.sharding import PartitionSpec as P

SWEEPS = 4

frequency = 1.0

MESH = pl.DeviceIdType.MESH


def spectral_rows(values):
    count = len(values)
    differences, products = {}, {}

    def product(coefficient, low, high):
        if (low, high) not in differences:
            differences[low, high] = values[low] - values[high]
        if (coefficient, low, high) not in products:
            products[coefficient, low, high] = coefficient * differences[low, high]
        return products[coefficient, low, high]

    rows = []
    for n in range(count):
        total = None
        for k in range(1, (count + 1) // 2):
            coefficient = frequency * 0.5 * (-1.0) ** k / math.tan(math.pi * k / count)
            a, b = (n - k) % count, (n + k) % count
            if a > b:
                a, b, coefficient = b, a, -coefficient
            if coefficient < 0:
                term, sign = product(-coefficient, a, b), -1
            else:
                term, sign = product(coefficient, a, b), 1
            if total is None:
                total = term if sign > 0 else -term
            else:
                total = total + term if sign > 0 else total - term
        rows.append(total)
    return rows


def lane_sum(cur, lane):
    size = cur.shape[-1]
    left = jnp.where(lane == 0, 0.0, pltpu.roll(cur, 1, 1))
    right = jnp.where(lane == size - 1, 0.0, pltpu.roll(cur, size - 1, 1))
    return left + right


def kernel(inst_size, cells_size, state, forcing, diffusion, blocks, out,
           home, force, weight, block, part, state_blk, part_blk, residual, source, update,
           edge, halo, final, load_sem, own_sem, send_a, recv_a, send_b, recv_b, send_x, recv_x,
           send_u, recv_u, send_r, recv_r, send_o, recv_o):
    me, cell = lax.axis_index("inst"), lax.axis_index("cells")
    own, variables, planes, height, lanes = state.shape
    rows = height // inst_size
    count = own * inst_size

    def peer(step):
        return lax.rem(me + step, inst_size)

    def row_block(i):
        return pl.ds(pl.multiple_of(i * rows, rows), rows)

    has_before, has_after = cell > 0, cell < cells_size - 1
    has_above, has_below = me > 0, me < inst_size - 1
    before, after = {"cells": cell - 1}, {"cells": cell + 1}
    above, below = {"inst": me - 1}, {"inst": me + 1}

    def remote(src, dst, send, recv, target):
        return pltpu.make_async_remote_copy(
            src_ref=src, dst_ref=dst, send_sem=send, recv_sem=recv,
            device_id=target, device_id_type=MESH)

    loads = [
        pltpu.make_async_copy(state, home.at[:, :, pl.ds(1, planes)], load_sem.at[0]),
        pltpu.make_async_copy(forcing, force, load_sem.at[1]),
        pltpu.make_async_copy(diffusion, weight, load_sem.at[2]),
        pltpu.make_async_copy(
            state.at[:, :, :, row_block(me)], state_blk.at[pl.ds(me * own, own)], load_sem.at[3]),
        pltpu.make_async_copy(blocks, block, load_sem.at[4]),
    ]
    for load in loads:
        load.start()

    zero_home = jnp.zeros((own, variables, height, lanes), jnp.float32)

    @pl.when(jnp.logical_not(has_before))
    def _():
        home[:, :, 0] = zero_home

    @pl.when(jnp.logical_not(has_after))
    def _():
        home[:, :, planes + 1] = zero_home

    for s in range(SWEEPS):
        zero_blk = jnp.zeros((count, variables, rows, lanes), jnp.float32)

        @pl.when(jnp.logical_not(has_before))
        def _():
            update[s, :, :, 0] = zero_blk

        @pl.when(jnp.logical_not(has_after))
        def _():
            update[s, :, :, planes + 1] = zero_blk

        zero_halo = jnp.zeros((variables, planes, count, lanes), jnp.float32)

        @pl.when(jnp.logical_not(has_above))
        def _():
            halo[s, 0] = zero_halo

        @pl.when(jnp.logical_not(has_below))
        def _():
            halo[s, 1] = zero_halo

    barrier = pltpu.get_barrier_semaphore()
    for step in range(1, inst_size):
        pl.semaphore_signal(barrier, 1, device_id={"inst": peer(step)}, device_id_type=MESH)

    @pl.when(has_before)
    def _():
        pl.semaphore_signal(barrier, 1, device_id=before, device_id_type=MESH)

    @pl.when(has_after)
    def _():
        pl.semaphore_signal(barrier, 1, device_id=after, device_id_type=MESH)

    ends = jnp.where(has_before, 1, 0) + jnp.where(has_after, 1, 0)
    pl.semaphore_wait(barrier, inst_size - 1 + ends)

    to_before = remote(state.at[:, :, 0], home.at[:, :, planes + 1],
                       send_x.at[0], recv_x.at[1], before)
    to_after = remote(state.at[:, :, planes - 1], home.at[:, :, 0],
                      send_x.at[1], recv_x.at[0], after)
    pl.when(has_before)(to_before.start)
    pl.when(has_after)(to_after.start)

    moves = []
    for step in range(1, inst_size):
        moves.append(remote(
            state.at[:, :, :, row_block(peer(step))], state_blk.at[pl.ds(me * own, own)],
            send_a.at[step], recv_a.at[step], {"inst": peer(step)}))
        moves[-1].start()

    for load in loads[:3]:
        load.wait()
    lane = lax.broadcasted_iota(jnp.int32, (height, lanes), 1)
    row = lax.broadcasted_iota(jnp.int32, (height, lanes), 0)

    def local_plane(x):
        w = weight[x]
        for n in range(own):
            for v in range(variables):
                cur = home[n, v, x + 1]
                beside = home[n, v, x] + home[n, v, x + 2] + lane_sum(cur, lane)
                beside = beside + jnp.where(row == 0, 0.0, pltpu.roll(cur, 1, 0))
                beside = beside + jnp.where(row == height - 1, 0.0, pltpu.roll(cur, height - 1, 0))
                part[n, v, x] = w * (6.0 * cur - beside) - force[n, v, x]

    pl.loop(1, planes - 1)(local_plane)

    @pl.when(has_before)
    def _():
        to_after.wait_recv()

    @pl.when(has_after)
    def _():
        to_before.wait_recv()

    pl.loop(0, 2)(lambda i: local_plane(i * (planes - 1)))

    chunks = ((0, 1), (planes - 1, 1), (1, planes - 2))
    own_parts = pltpu.make_async_copy(
        part.at[:, :, :, row_block(me)], part_blk.at[pl.ds(me * own, own)], own_sem.at[0])
    own_parts.start()
    parts = [[] for _ in chunks]
    for c, (first, size) in enumerate(chunks):
        for step in range(1, inst_size):
            parts[c].append(remote(
                part.at[:, :, pl.ds(first, size), row_block(peer(step))],
                part_blk.at[pl.ds(me * own, own), :, pl.ds(first, size)],
                send_b.at[c, step], recv_b.at[c, step], {"inst": peer(step)}))
            parts[c][-1].start()

    loads[3].wait()
    loads[4].wait()
    own_parts.wait()
    lane = lax.broadcasted_iota(jnp.int32, (rows, lanes), 1)
    row = lax.broadcasted_iota(jnp.int32, (rows, lanes), 0)

    def apply(x, read, write):
        b = [[block[v, u, x] for u in range(variables)] for v in range(variables)]
        for n in range(count):
            src = [read(n, u) for u in range(variables)]
            for v in range(variables):
                total = b[v][0] * src[0]
                for u in range(1, variables):
                    total = total + b[v][u] * src[u]
                write(n, v, total)

    def keep(s, x):
        def write(n, v, value):
            update[s, n, v, x + 1] = value
            edge[s, 0, v, x, n:n + 1] = value[rows - 1:rows]
            edge[s, 1, v, x, n:n + 1] = value[0:1]
        return write

    def finish(x):
        def write(n, v, value):
            final[n, v, x] = state_blk[n, v, x] + value
        return write

    def first_plane(x):
        for v in range(variables):
            coupled = spectral_rows([state_blk[n, v, x] for n in range(count)])
            for n in range(count):
                residual[n, v, x] = -(part_blk[n, v, x] + coupled[n])
        apply(x, lambda n, u: residual[n, u, x], keep(0, x))

    def sweep_plane(s, x, writer):
        w = weight[x, row_block(me)]
        for v in range(variables):
            values = [update[s, n, v, x + 1] for n in range(count)]
            coupled = spectral_rows(values)
            for n in range(count):
                cur = values[n]
                beside = update[s, n, v, x] + update[s, n, v, x + 2] + lane_sum(cur, lane)
                over = pltpu.roll(cur, 1, 0)
                under = pltpu.roll(cur, rows - 1, 0)
                beside = beside + jnp.where(row == 0, halo[s, 0, v, x, n:n + 1], over)
                beside = beside + jnp.where(row == rows - 1, halo[s, 1, v, x, n:n + 1], under)
                source[n, v] = residual[n, v, x] - coupled[n] + w * beside
        apply(x, lambda n, u: source[n, u], writer)

    sent_x, sent_rows = [], []

    def start_planes(s):
        back = remote(update.at[s, :, :, 1], update.at[s, :, :, planes + 1],
                      send_u.at[s, 0], recv_u.at[s, 1], before)
        on = remote(update.at[s, :, :, planes], update.at[s, :, :, 0],
                    send_u.at[s, 1], recv_u.at[s, 0], after)
        pl.when(has_before)(back.start)
        pl.when(has_after)(on.start)
        sent_x.append((back, on))

    def start_rows(s):
        down = remote(edge.at[s, 0], halo.at[s, 0], send_r.at[s, 0], recv_r.at[s, 0], below)
        up = remote(edge.at[s, 1], halo.at[s, 1], send_r.at[s, 1], recv_r.at[s, 1], above)
        pl.when(has_below)(down.start)
        pl.when(has_above)(up.start)
        sent_rows.append((down, up))

    for move in moves + parts[0] + parts[1]:
        move.wait_recv()
    pl.loop(0, 2)(lambda i: first_plane(i * (planes - 1)))
    start_planes(0)
    for move in parts[2]:
        move.wait_recv()
    pl.loop(1, planes - 1)(first_plane)
    start_rows(0)

    returns = []

    def start_return(c, first, size):
        for step in range(1, inst_size):
            returns.append(remote(
                final.at[pl.ds(peer(step) * own, own), :, pl.ds(first, size)],
                out.at[:, :, pl.ds(first, size), row_block(me)],
                send_o.at[c, step], recv_o.at[c, step], {"inst": peer(step)}))
            returns[-1].start()

    half = planes // 2
    for s in range(SWEEPS):
        last = s == SWEEPS - 1
        down, up = sent_rows[s]
        pl.when(has_above)(down.wait_recv)
        pl.when(has_below)(up.wait_recv)

        def one(x):
            sweep_plane(s, x, finish(x) if last else keep(s + 1, x))

        if last:
            pl.loop(1, half)(one)
            start_return(0, 1, half - 1)
            pl.loop(half, planes - 1)(one)
            start_return(1, half, planes - 1 - half)
        else:
            pl.loop(1, planes - 1)(one)
        back, on = sent_x[s]
        pl.when(has_before)(on.wait_recv)
        pl.when(has_after)(back.wait_recv)
        pl.loop(0, 2)(lambda i: one(i * (planes - 1)))
        if last:
            start_return(2, 0, 1)
            start_return(3, planes - 1, 1)
        else:
            start_planes(s + 1)
            start_rows(s + 1)

    own_out = pltpu.make_async_copy(
        final.at[pl.ds(me * own, own)], out.at[:, :, :, row_block(me)], own_sem.at[1])
    own_out.start()
    for move in moves + parts[0] + parts[1] + parts[2]:
        move.wait_send()
    for back, on in [(to_before, to_after)] + sent_x:
        pl.when(has_before)(back.wait_send)
        pl.when(has_after)(on.wait_send)
    for down, up in sent_rows:
        pl.when(has_below)(down.wait_send)
        pl.when(has_above)(up.wait_send)
    own_out.wait()
    for move in returns:
        move.wait()


def on_device(flow_state, forcing, diffusion, block_inverse):
    inst_size, cells_size = lax.axis_size("inst"), lax.axis_size("cells")
    own, variables, planes, height, lanes = flow_state.shape
    count, rows = own * inst_size, height // inst_size
    f32 = jnp.float32
    dma = pltpu.SemaphoreType.DMA
    block_field = (count, variables, planes, rows, lanes)
    scratch = [
        pltpu.VMEM((own, variables, planes + 2, height, lanes), f32),
        pltpu.VMEM(forcing.shape, f32),
        pltpu.VMEM(diffusion.shape, f32),
        pltpu.VMEM(block_inverse.shape, f32),
        pltpu.VMEM(flow_state.shape, f32),
        pltpu.VMEM(block_field, f32),
        pltpu.VMEM(block_field, f32),
        pltpu.VMEM(block_field, f32),
        pltpu.VMEM((count, variables, rows, lanes), f32),
        pltpu.VMEM((SWEEPS, count, variables, planes + 2, rows, lanes), f32),
        pltpu.VMEM((SWEEPS, 2, variables, planes, count, lanes), f32),
        pltpu.VMEM((SWEEPS, 2, variables, planes, count, lanes), f32),
        pltpu.VMEM(block_field, f32),
        dma((5,)), dma((2,)),
        dma((inst_size,)), dma((inst_size,)),
        dma((3, inst_size)), dma((3, inst_size)),
        dma((2,)), dma((2,)),
        dma((SWEEPS, 2)), dma((SWEEPS, 2)),
        dma((SWEEPS, 2)), dma((SWEEPS, 2)),
        dma((4, inst_size)), dma((4, inst_size)),
    ]
    return pl.pallas_call(
        functools.partial(kernel, inst_size, cells_size),
        out_shape=jax.ShapeDtypeStruct(flow_state.shape, f32),
        in_specs=[pl.BlockSpec(memory_space=pl.ANY)] * 4,
        out_specs=pl.BlockSpec(memory_space=pl.ANY),
        scratch_shapes=scratch,
        compiler_params=pltpu.CompilerParams(collective_id=0, has_side_effects=True),
    )(flow_state, forcing, diffusion, block_inverse)


def solution(mesh):
    in_specs = (
        P("inst", None, "cells", None, None),
        P("inst", None, "cells", None, None),
        P("cells", None, None),
        P(None, None, "cells", "inst", None),
    )
    out_specs = P("inst", None, "cells", None, None)
    return jax.shard_map(
        on_device, mesh=mesh, in_specs=in_specs, out_specs=out_specs, check_vma=False
    )
```

time: 185 us -> 78.1 us (0.42); the launches traced: 182 us -> 77.9 us
  Pallas kernels: 0 us -> 75.5 us
  waiting for transfers between devices: 61.4 us -> 0 us
  starting transfers between devices: 55.7 us -> 0 us
  other arithmetic: 25.7 us -> 0 us
  blocking collectives: 18.5 us -> 0 us
  matrix products: 10.2 us -> 0 us
  local copies, waits for them, and re-layouts: 9.69 us -> 2.47 us
    pallas_call x0 -> x1, Pallas kernels: none -> 75.5 us  [on_device(): pl.pallas_call(functools.partial(kernel, inst_size, cells_size), out_shap...]
    ppermute x18 -> x0, starting transfers between devices: 45.8 us -> none  [the longest x9 26.1 us: extended(): before = lax.ppermute(last, axis, up)]
    ppermute x18 -> x0, waiting for transfers between devices: 45.8 us -> none  [the longest x9 23.4 us: extended(): after = lax.ppermute(initial, axis, down)]
    all_to_all x1 -> x0, blocking collectives: 18.5 us -> none  [on_device(): lax.all_to_all(moved_state + update, 'inst', split_axis=0, concat_axis=3,...]
    all_to_all x2 -> x0, waiting for transfers between devices: 15.6 us -> none  [the longest x1 15.6 us: on_device(): lax.all_to_all(local_part, 'inst', split_axis=3, concat_axis=0, tiled=True)]
    concatenate x9 -> x0, other arithmetic: 15.4 us -> none  [extended(): shard = jnp.concatenate([before, shard, after], axis=dim)]
    dot_general x5 -> x0, matrix products: 10.2 us -> none  [spectral_term(): product = jnp.dot(matrix, flat, precision=lax.Precision.HIGHEST)]
    all_to_all x2 -> x0, starting transfers between devices: 9.88 us -> none  [the longest x1 5.57 us: on_device(): lax.all_to_all(local_part, 'inst', split_axis=3, concat_axis=0, tiled=True)]
  transfers between devices with their start and end apart: 20 -> 0, of which waited for: 15 -> 0; matrix products, arithmetic and copies ran while one was open for 6% -> 0% of each run, Pallas kernels for 0% -> 0%
where the time goes in v1:
time: 78.1 us; the launch traced here: 77.9 us
  Pallas kernels  75.5 us (97%)
  local copies, waits for them, and re-layouts  2.47 us (3%)
    pallas_call x1, Pallas kernels, on_device(): pl.pallas_call(functools.partial(kernel, inst_size, cells_size), out_shap...  75.5 us
    unnamed x1, local copies, waits for them, and re-layouts  2.47 us

profile of v1, /device:TPU:19, one launch (start us, length us, event | category | flops | bytes accessed | tf_op | source)
XLA Modules:
  0.0 77.9 jit_solution(5321893986306521612)
XLA Ops:
  0.0 75.5 %shard_map.46 = f32[2,5,8,32,128]{4,3,2,1,0:T(8,128)} custom-call(f32[2,5,8,32,128]{4,3,2,1,0:T(8,128)} %state.1, f32[2,5,8,32,128]{4,3,2,1,0:T(8,128)} %forcing.1, f32[8,32,128]{2,1,0:T(8,128)} %diffusion.1, f32[5,5,8,8,128]{4,3,2,1,0:T(8,128)} %blocks.1), custom_call_target="tpu_custom_call" | custom-call | tf_op jit(solution)/shard_map/pallas_call | solution.py:352
  75.5 2.5 %copy.6 = f32[2,5,8,32,128]{4,3,2,1,0:T(8,128)} copy(f32[2,5,8,32,128]{4,3,2,1,0:T(8,128)} %shard_map.46) | data formatting | bytes 2621440

commit v2 on v1

--- a/solution.py
+++ b/solution.py
@@ -154,7 +154,7 @@
     lane = lax.broadcasted_iota(jnp.int32, (height, lanes), 1)
     row = lax.broadcasted_iota(jnp.int32, (height, lanes), 0)
 
-    def local_plane(x):
+    def local_plane(x, p):
         w = weight[x]
         for n in range(own):
             for v in range(variables):
@@ -162,9 +162,21 @@
                 beside = home[n, v, x] + home[n, v, x + 2] + lane_sum(cur, lane)
                 beside = beside + jnp.where(row == 0, 0.0, pltpu.roll(cur, 1, 0))
                 beside = beside + jnp.where(row == height - 1, 0.0, pltpu.roll(cur, height - 1, 0))
-                part[n, v, x] = w * (6.0 * cur - beside) - force[n, v, x]
-
-    pl.loop(1, planes - 1)(local_plane)
+                part[n, v, p] = w * (6.0 * cur - beside) - force[n, v, x]
+
+    half = planes // 2
+
+    def outermost(one):
+        pl.loop(0, 2)(lambda i: one(i * (planes - 1), i))
+
+    def second(one):
+        pl.loop(0, 2)(lambda i: one(1 + i * (planes - 3), 2 + i))
+
+    def inner(first, end, one):
+        pl.loop(first, end)(lambda x: one(x, x + 2))
+
+    second(local_plane)
+    inner(2, planes - 2, local_plane)
 
     @pl.when(has_before)
     def _():
@@ -174,21 +186,25 @@
     def _():
         to_before.wait_recv()
 
-    pl.loop(0, 2)(lambda i: local_plane(i * (planes - 1)))
-
-    chunks = ((0, 1), (planes - 1, 1), (1, planes - 2))
+    outermost(local_plane)
+
     own_parts = pltpu.make_async_copy(
         part.at[:, :, :, row_block(me)], part_blk.at[pl.ds(me * own, own)], own_sem.at[0])
     own_parts.start()
-    parts = [[] for _ in chunks]
-    for c, (first, size) in enumerate(chunks):
+    ends_of = (0, 2, 4, half + 2, planes)
+    parts = [[] for _ in ends_of[1:]]
+
+    def start_part(c):
+        positions = pl.ds(ends_of[c], ends_of[c + 1] - ends_of[c])
         for step in range(1, inst_size):
             parts[c].append(remote(
-                part.at[:, :, pl.ds(first, size), row_block(peer(step))],
-                part_blk.at[pl.ds(me * own, own), :, pl.ds(first, size)],
+                part.at[:, :, positions, row_block(peer(step))],
+                part_blk.at[pl.ds(me * own, own), :, positions],
                 send_b.at[c, step], recv_b.at[c, step], {"inst": peer(step)}))
             parts[c][-1].start()
 
+    for c in range(3):
+        start_part(c)
     loads[3].wait()
     loads[4].wait()
     own_parts.wait()
@@ -205,11 +221,11 @@
                     total = total + b[v][u] * src[u]
                 write(n, v, total)
 
-    def keep(s, x):
+    def keep(s, x, p):
         def write(n, v, value):
             update[s, n, v, x + 1] = value
-            edge[s, 0, v, x, n:n + 1] = value[rows - 1:rows]
-            edge[s, 1, v, x, n:n + 1] = value[0:1]
+            edge[s, 0, v, p, n:n + 1] = value[rows - 1:rows]
+            edge[s, 1, v, p, n:n + 1] = value[0:1]
         return write
 
     def finish(x):
@@ -217,14 +233,14 @@
             final[n, v, x] = state_blk[n, v, x] + value
         return write
 
-    def first_plane(x):
+    def first_plane(x, p):
         for v in range(variables):
             coupled = spectral_rows([state_blk[n, v, x] for n in range(count)])
             for n in range(count):
-                residual[n, v, x] = -(part_blk[n, v, x] + coupled[n])
-        apply(x, lambda n, u: residual[n, u, x], keep(0, x))
-
-    def sweep_plane(s, x, writer):
+                residual[n, v, x] = -(part_blk[n, v, p] + coupled[n])
+        apply(x, lambda n, u: residual[n, u, x], keep(0, x, p))
+
+    def sweep_plane(s, x, p, writer):
         w = weight[x, row_block(me)]
         for v in range(variables):
             values = [update[s, n, v, x + 1] for n in range(count)]
@@ -234,12 +250,12 @@
                 beside = update[s, n, v, x] + update[s, n, v, x + 2] + lane_sum(cur, lane)
                 over = pltpu.roll(cur, 1, 0)
                 under = pltpu.roll(cur, rows - 1, 0)
-                beside = beside + jnp.where(row == 0, halo[s, 0, v, x, n:n + 1], over)
-                beside = beside + jnp.where(row == rows - 1, halo[s, 1, v, x, n:n + 1], under)
+                beside = beside + jnp.where(row == 0, halo[s, 0, v, p, n:n + 1], over)
+                beside = beside + jnp.where(row == rows - 1, halo[s, 1, v, p, n:n + 1], under)
                 source[n, v] = residual[n, v, x] - coupled[n] + w * beside
         apply(x, lambda n, u: source[n, u], writer)
 
-    sent_x, sent_rows = [], []
+    sent_x, sent_rows = [], {}
 
     def start_planes(s):
         back = remote(update.at[s, :, :, 1], update.at[s, :, :, planes + 1],
@@ -250,21 +266,69 @@
         pl.when(has_after)(on.start)
         sent_x.append((back, on))
 
-    def start_rows(s):
-        down = remote(edge.at[s, 0], halo.at[s, 0], send_r.at[s, 0], recv_r.at[s, 0], below)
-        up = remote(edge.at[s, 1], halo.at[s, 1], send_r.at[s, 1], recv_r.at[s, 1], above)
+    def wait_planes(s):
+        back, on = sent_x[s]
+        pl.when(has_before)(on.wait_recv)
+        pl.when(has_after)(back.wait_recv)
+
+    def start_rows(s, g):
+        positions = pl.ds(0, 2) if g == 0 else pl.ds(2, planes - 2)
+        down = remote(edge.at[s, 0, :, positions], halo.at[s, 0, :, positions],
+                      send_r.at[s, g, 0], recv_r.at[s, g, 0], below)
+        up = remote(edge.at[s, 1, :, positions], halo.at[s, 1, :, positions],
+                    send_r.at[s, g, 1], recv_r.at[s, g, 1], above)
         pl.when(has_below)(down.start)
         pl.when(has_above)(up.start)
-        sent_rows.append((down, up))
-
-    for move in moves + parts[0] + parts[1]:
+        sent_rows[s, g] = (down, up)
+
+    def wait_rows(s, g):
+        down, up = sent_rows[s, g]
+        pl.when(has_above)(down.wait_recv)
+        pl.when(has_below)(up.wait_recv)
+
+    def wait_part(c):
+        for move in parts[c]:
+            move.wait_recv()
+
+    def swept(s):
+        return lambda x, p: sweep_plane(s, x, p, keep(s + 1, x, p))
+
+    def sweep_outermost(s):
+        wait_planes(s)
+        wait_rows(s, 0)
+        outermost(swept(s))
+        start_planes(s + 1)
+        start_rows(s + 1, 0)
+
+    def sweep_others(s):
+        wait_rows(s, 1)
+        second(swept(s))
+        inner(2, planes - 2, swept(s))
+        start_rows(s + 1, 1)
+
+    for move in moves:
         move.wait_recv()
-    pl.loop(0, 2)(lambda i: first_plane(i * (planes - 1)))
+    wait_part(0)
+    outermost(first_plane)
     start_planes(0)
-    for move in parts[2]:
-        move.wait_recv()
-    pl.loop(1, planes - 1)(first_plane)
-    start_rows(0)
+    start_rows(0, 0)
+    start_part(3)
+    wait_part(1)
+    second(first_plane)
+    wait_part(2)
+    inner(2, half, first_plane)
+    sweep_outermost(0)
+    wait_part(3)
+    inner(half, planes - 2, first_plane)
+    start_rows(0, 1)
+    sweep_others(0)
+    for s in range(1, SWEEPS - 1):
+        if s < SWEEPS - 2:
+            sweep_outermost(s)
+            sweep_others(s)
+        else:
+            sweep_others(s)
+            sweep_outermost(s)
 
     returns = []
 
@@ -276,43 +340,34 @@
                 send_o.at[c, step], recv_o.at[c, step], {"inst": peer(step)}))
             returns[-1].start()
 
-    half = planes // 2
-    for s in range(SWEEPS):
-        last = s == SWEEPS - 1
-        down, up = sent_rows[s]
-        pl.when(has_above)(down.wait_recv)
-        pl.when(has_below)(up.wait_recv)
-
-        def one(x):
-            sweep_plane(s, x, finish(x) if last else keep(s + 1, x))
-
-        if last:
-            pl.loop(1, half)(one)
-            start_return(0, 1, half - 1)
-            pl.loop(half, planes - 1)(one)
-            start_return(1, half, planes - 1 - half)
-        else:
-            pl.loop(1, planes - 1)(one)
-        back, on = sent_x[s]
-        pl.when(has_before)(on.wait_recv)
-        pl.when(has_after)(back.wait_recv)
-        pl.loop(0, 2)(lambda i: one(i * (planes - 1)))
-        if last:
-            start_return(2, 0, 1)
-            start_return(3, planes - 1, 1)
-        else:
-            start_planes(s + 1)
-            start_rows(s + 1)
+    s = SWEEPS - 1
+
+    def last(x, p):
+        sweep_plane(s, x, p, finish(x))
+
+    wait_rows(s, 1)
+    inner(2, half, last)
+    start_return(0, 2, half - 2)
+    inner(half, planes - 2, last)
+    start_return(1, half, planes - 2 - half)
+    second(last)
+    start_return(2, 1, 1)
+    start_return(3, planes - 2, 1)
+    wait_planes(s)
+    wait_rows(s, 0)
+    outermost(last)
+    start_return(4, 0, 1)
+    start_return(5, planes - 1, 1)
 
     own_out = pltpu.make_async_copy(
         final.at[pl.ds(me * own, own)], out.at[:, :, :, row_block(me)], own_sem.at[1])
     own_out.start()
-    for move in moves + parts[0] + parts[1] + parts[2]:
+    for move in moves + sum(parts, []):
         move.wait_send()
     for back, on in [(to_before, to_after)] + sent_x:
         pl.when(has_before)(back.wait_send)
         pl.when(has_after)(on.wait_send)
-    for down, up in sent_rows:
+    for down, up in sent_rows.values():
         pl.when(has_below)(down.wait_send)
         pl.when(has_above)(up.wait_send)
     own_out.wait()
@@ -343,11 +398,11 @@
         pltpu.VMEM(block_field, f32),
         dma((5,)), dma((2,)),
         dma((inst_size,)), dma((inst_size,)),
-        dma((3, inst_size)), dma((3, inst_size)),
+        dma((4, inst_size)), dma((4, inst_size)),
         dma((2,)), dma((2,)),
         dma((SWEEPS, 2)), dma((SWEEPS, 2)),
-        dma((SWEEPS, 2)), dma((SWEEPS, 2)),
-        dma((4, inst_size)), dma((4, inst_size)),
+        dma((SWEEPS, 2, 2)), dma((SWEEPS, 2, 2)),
+        dma((6, inst_size)), dma((6, inst_size)),
     ]
     return pl.pallas_call(
         functools.partial(kernel, inst_size, cells_size),

time: 78.1 us -> 71.7 us (0.918)
  Pallas kernels: 75.5 us -> 69.1 us
    pallas_call x1, Pallas kernels: 75.5 us -> 69.1 us  [on_device(): pl.pallas_call(functools.partial(kernel, inst_size, cells_size), out_shap...]
where the time goes in v2:
time: 71.7 us; the launch traced here: 71.6 us
  Pallas kernels  69.1 us (96%)
  local copies, waits for them, and re-layouts  2.47 us (3%)
    pallas_call x1, Pallas kernels, on_device(): pl.pallas_call(functools.partial(kernel, inst_size, cells_size), out_shap...  69.1 us
    unnamed x1, local copies, waits for them, and re-layouts  2.47 us

profile of v2, /device:TPU:19, one launch (start us, length us, event | category | flops | bytes accessed | tf_op | source)
XLA Modules:
  0.0 71.6 jit_solution(15147702255717493459)
XLA Ops:
  0.0 69.1 %shard_map.46 = f32[2,5,8,32,128]{4,3,2,1,0:T(8,128)} custom-call(f32[2,5,8,32,128]{4,3,2,1,0:T(8,128)} %state.1, f32[2,5,8,32,128]{4,3,2,1,0:T(8,128)} %forcing.1, f32[8,32,128]{2,1,0:T(8,128)} %diffusion.1, f32[5,5,8,8,128]{4,3,2,1,0:T(8,128)} %blocks.1), custom_call_target="tpu_custom_call" | custom-call | tf_op jit(solution)/shard_map/pallas_call | solution.py:407
  69.1 2.5 %copy.6 = f32[2,5,8,32,128]{4,3,2,1,0:T(8,128)} copy(f32[2,5,8,32,128]{4,3,2,1,0:T(8,128)} %shard_map.46) | data formatting | bytes 2621440

commit v3 on v2

--- a/solution.py
+++ b/solution.py
@@ -142,19 +142,28 @@
     pl.when(has_before)(to_before.start)
     pl.when(has_after)(to_after.start)
 
-    moves = []
-    for step in range(1, inst_size):
-        moves.append(remote(
-            state.at[:, :, :, row_block(peer(step))], state_blk.at[pl.ds(me * own, own)],
-            send_a.at[step], recv_a.at[step], {"inst": peer(step)}))
-        moves[-1].start()
+    half = planes // 2
+    pieces = ((0, half), (planes - 2, 2), (half, planes - 2 - half))
+    moves = [[] for _ in pieces]
+
+    def start_state(c):
+        first, size = pieces[c]
+        for step in range(1, inst_size):
+            moves[c].append(remote(
+                state.at[:, :, pl.ds(first, size), row_block(peer(step))],
+                state_blk.at[pl.ds(me * own, own), :, pl.ds(first, size)],
+                send_a.at[c, step], recv_a.at[c, step], {"inst": peer(step)}))
+            moves[c][-1].start()
+
+    start_state(0)
+    start_state(1)
 
     for load in loads[:3]:
         load.wait()
     lane = lax.broadcasted_iota(jnp.int32, (height, lanes), 1)
     row = lax.broadcasted_iota(jnp.int32, (height, lanes), 0)
 
-    def local_plane(x, p):
+    def local_plane(x, p, q):
         w = weight[x]
         for n in range(own):
             for v in range(variables):
@@ -164,16 +173,14 @@
                 beside = beside + jnp.where(row == height - 1, 0.0, pltpu.roll(cur, height - 1, 0))
                 part[n, v, p] = w * (6.0 * cur - beside) - force[n, v, x]
 
-    half = planes // 2
-
     def outermost(one):
-        pl.loop(0, 2)(lambda i: one(i * (planes - 1), i))
+        pl.loop(0, 2)(lambda i: one(i * (planes - 1), i, i))
 
     def second(one):
-        pl.loop(0, 2)(lambda i: one(1 + i * (planes - 3), 2 + i))
+        pl.loop(0, 2)(lambda i: one(1 + i * (planes - 3), 2 + i, 2 + i * (planes - 3)))
 
     def inner(first, end, one):
-        pl.loop(first, end)(lambda x: one(x, x + 2))
+        pl.loop(first, end)(lambda x: one(x, x + 2, x + 1))
 
     second(local_plane)
     inner(2, planes - 2, local_plane)
@@ -203,8 +210,10 @@
                 send_b.at[c, step], recv_b.at[c, step], {"inst": peer(step)}))
             parts[c][-1].start()
 
-    for c in range(3):
-        start_part(c)
+    start_part(0)
+    start_state(2)
+    start_part(1)
+    start_part(2)
     loads[3].wait()
     loads[4].wait()
     own_parts.wait()
@@ -221,11 +230,11 @@
                     total = total + b[v][u] * src[u]
                 write(n, v, total)
 
-    def keep(s, x, p):
+    def keep(s, x, q):
         def write(n, v, value):
             update[s, n, v, x + 1] = value
-            edge[s, 0, v, p, n:n + 1] = value[rows - 1:rows]
-            edge[s, 1, v, p, n:n + 1] = value[0:1]
+            edge[s, 0, v, q, n:n + 1] = value[rows - 1:rows]
+            edge[s, 1, v, q, n:n + 1] = value[0:1]
         return write
 
     def finish(x):
@@ -233,14 +242,14 @@
             final[n, v, x] = state_blk[n, v, x] + value
         return write
 
-    def first_plane(x, p):
+    def first_plane(x, p, q):
         for v in range(variables):
             coupled = spectral_rows([state_blk[n, v, x] for n in range(count)])
             for n in range(count):
                 residual[n, v, x] = -(part_blk[n, v, p] + coupled[n])
-        apply(x, lambda n, u: residual[n, u, x], keep(0, x, p))
-
-    def sweep_plane(s, x, p, writer):
+        apply(x, lambda n, u: residual[n, u, x], keep(0, x, q))
+
+    def sweep_plane(s, x, q, writer):
         w = weight[x, row_block(me)]
         for v in range(variables):
             values = [update[s, n, v, x + 1] for n in range(count)]
@@ -250,8 +259,8 @@
                 beside = update[s, n, v, x] + update[s, n, v, x + 2] + lane_sum(cur, lane)
                 over = pltpu.roll(cur, 1, 0)
                 under = pltpu.roll(cur, rows - 1, 0)
-                beside = beside + jnp.where(row == 0, halo[s, 0, v, p, n:n + 1], over)
-                beside = beside + jnp.where(row == rows - 1, halo[s, 1, v, p, n:n + 1], under)
+                beside = beside + jnp.where(row == 0, halo[s, 0, v, q, n:n + 1], over)
+                beside = beside + jnp.where(row == rows - 1, halo[s, 1, v, q, n:n + 1], under)
                 source[n, v] = residual[n, v, x] - coupled[n] + w * beside
         apply(x, lambda n, u: source[n, u], writer)
 
@@ -271,8 +280,10 @@
         pl.when(has_before)(on.wait_recv)
         pl.when(has_after)(back.wait_recv)
 
+    row_ends = (0, 2, half + 1, planes)
+
     def start_rows(s, g):
-        positions = pl.ds(0, 2) if g == 0 else pl.ds(2, planes - 2)
+        positions = pl.ds(row_ends[g], row_ends[g + 1] - row_ends[g])
         down = remote(edge.at[s, 0, :, positions], halo.at[s, 0, :, positions],
                       send_r.at[s, g, 0], recv_r.at[s, g, 0], below)
         up = remote(edge.at[s, 1, :, positions], halo.at[s, 1, :, positions],
@@ -290,8 +301,12 @@
         for move in parts[c]:
             move.wait_recv()
 
+    def wait_state(c):
+        for move in moves[c]:
+            move.wait_recv()
+
     def swept(s):
-        return lambda x, p: sweep_plane(s, x, p, keep(s + 1, x, p))
+        return lambda x, p, q: sweep_plane(s, x, q, keep(s + 1, x, q))
 
     def sweep_outermost(s):
         wait_planes(s)
@@ -302,12 +317,14 @@
 
     def sweep_others(s):
         wait_rows(s, 1)
-        second(swept(s))
-        inner(2, planes - 2, swept(s))
+        inner(1, half, swept(s))
         start_rows(s + 1, 1)
-
-    for move in moves:
-        move.wait_recv()
+        wait_rows(s, 2)
+        inner(half, planes - 1, swept(s))
+        start_rows(s + 1, 2)
+
+    wait_state(0)
+    wait_state(1)
     wait_part(0)
     outermost(first_plane)
     start_planes(0)
@@ -317,18 +334,17 @@
     second(first_plane)
     wait_part(2)
     inner(2, half, first_plane)
+    start_rows(0, 1)
     sweep_outermost(0)
+    wait_state(2)
     wait_part(3)
     inner(half, planes - 2, first_plane)
-    start_rows(0, 1)
+    start_rows(0, 2)
     sweep_others(0)
-    for s in range(1, SWEEPS - 1):
-        if s < SWEEPS - 2:
-            sweep_outermost(s)
-            sweep_others(s)
-        else:
-            sweep_others(s)
-            sweep_outermost(s)
+    for s in range(1, SWEEPS - 2):
+        sweep_outermost(s)
+        sweep_others(s)
+    sweep_others(SWEEPS - 2)
 
     returns = []
 
@@ -342,14 +358,16 @@
 
     s = SWEEPS - 1
 
-    def last(x, p):
-        sweep_plane(s, x, p, finish(x))
+    def last(x, p, q):
+        sweep_plane(s, x, q, finish(x))
 
     wait_rows(s, 1)
     inner(2, half, last)
     start_return(0, 2, half - 2)
+    wait_rows(s, 2)
     inner(half, planes - 2, last)
     start_return(1, half, planes - 2 - half)
+    sweep_outermost(s - 1)
     second(last)
     start_return(2, 1, 1)
     start_return(3, planes - 2, 1)
@@ -362,7 +380,7 @@
     own_out = pltpu.make_async_copy(
         final.at[pl.ds(me * own, own)], out.at[:, :, :, row_block(me)], own_sem.at[1])
     own_out.start()
-    for move in moves + sum(parts, []):
+    for move in sum(moves + parts, []):
         move.wait_send()
     for back, on in [(to_before, to_after)] + sent_x:
         pl.when(has_before)(back.wait_send)
@@ -397,11 +415,11 @@
         pltpu.VMEM((SWEEPS, 2, variables, planes, count, lanes), f32),
         pltpu.VMEM(block_field, f32),
         dma((5,)), dma((2,)),
-        dma((inst_size,)), dma((inst_size,)),
+        dma((3, inst_size)), dma((3, inst_size)),
         dma((4, inst_size)), dma((4, inst_size)),
         dma((2,)), dma((2,)),
         dma((SWEEPS, 2)), dma((SWEEPS, 2)),
-        dma((SWEEPS, 2, 2)), dma((SWEEPS, 2, 2)),
+        dma((SWEEPS, 3, 2)), dma((SWEEPS, 3, 2)),
         dma((6, inst_size)), dma((6, inst_size)),
     ]
     return pl.pallas_call(

time: 71.7 us -> 67.9 us (0.947)
  the two profiles are of different devices: /device:TPU:19 before, /device:TPU:11 now
where the time goes in v3:
time: 67.9 us; the launch traced here: 67.7 us
  Pallas kernels  65.2 us (96%)
  local copies, waits for them, and re-layouts  2.47 us (4%)
    pallas_call x1, Pallas kernels, on_device(): pl.pallas_call(functools.partial(kernel, inst_size, cells_size), out_shap...  65.2 us
    unnamed x1, local copies, waits for them, and re-layouts  2.47 us

profile of v3, /device:TPU:11, one launch (start us, length us, event | category | flops | bytes accessed | tf_op | source)
XLA Modules:
  0.0 67.7 jit_solution(17039915889259404914)
XLA Ops:
  0.0 65.2 %shard_map.46 = f32[2,5,8,32,128]{4,3,2,1,0:T(8,128)} custom-call(f32[2,5,8,32,128]{4,3,2,1,0:T(8,128)} %state.1, f32[2,5,8,32,128]{4,3,2,1,0:T(8,128)} %forcing.1, f32[8,32,128]{2,1,0:T(8,128)} %diffusion.1, f32[5,5,8,8,128]{4,3,2,1,0:T(8,128)} %blocks.1), custom_call_target="tpu_custom_call" | custom-call | tf_op jit(solution)/shard_map/pallas_call | solution.py:425
  65.3 2.5 %copy.6 = f32[2,5,8,32,128]{4,3,2,1,0:T(8,128)} copy(f32[2,5,8,32,128]{4,3,2,1,0:T(8,128)} %shard_map.46) | data formatting | bytes 2621440
